TPU v7x, 32 devices: a whole 2x2x4 slice. The times are simulated.
32 devices in a mesh: groups: 2 (over y), dp: 4 (over z), tensor: 4 (over x, core).
Axes of the slice: x: 2, y: 2, z: 4, core: 2. Of those that a mesh axis runs over, the one named last changes fastest.
Arguments:
- tokens: bfloat16 [4096, 4096], P(('groups', 'dp')), parts along dimension 0, may hold values from -6 to 6
- w_query: bfloat16 [4096, 4096], P('dp', 'tensor'), may hold values from -0.09375 to 0.09375
- w_key: bfloat16 [4096, 1024], P('dp', 'tensor'), may hold values from -0.09375 to 0.09375
- w_value: bfloat16 [4096, 1024], P('dp', 'tensor'), may hold values from -0.09375 to 0.09375
- a_query: bfloat16 [8, 4096, 32], P(('groups', 'dp'), 'tensor'), parts along dimension 0, may hold values from -0.09375 to 0.09375
- b_query: bfloat16 [8, 32, 4096], P(('groups', 'dp'), None, 'tensor'), parts along dimension 0, may hold values from -1 to 1
- a_value: bfloat16 [8, 4096, 32], P(('groups', 'dp'), 'tensor'), parts along dimension 0, may hold values from -0.09375 to 0.09375
- b_value: bfloat16 [8, 32, 1024], P(('groups', 'dp'), None, 'tensor'), parts along dimension 0, may hold values from -1 to 1
- adapter_ranks: int32 [8], P('groups'), parts along dimension 0, may hold values from 16 to 32
- adapter_slot: int32 [4], replicated, may hold values from 0 to 3, each once
- block_adapter: int32 [32, 1], P(('groups', 'dp')), parts along dimension 0, may hold values from 0 to 3
- live_tokens: int32 [8], P(('groups', 'dp')), parts along dimension 0, may hold values from 1 to 512, 1280 in all
- d_heads: bfloat16 [4096, 4096], P(('groups', 'dp'), 'tensor'), parts along dimension 0, may hold values from -0.29882812 to 0.29882812
Outputs:
- grad_a_query: float32 [8, 4096, 32], P(('groups', 'dp'), 'tensor'), parts along dimension 0
- grad_b_query: float32 [8, 32, 4096], P(('groups', 'dp'), None, 'tensor'), parts along dimension 0
- grad_a_value: float32 [8, 4096, 32], P(('groups', 'dp'), 'tensor'), parts along dimension 0
- grad_b_value: float32 [8, 32, 1024], P(('groups', 'dp'), None, 'tensor'), parts along dimension 0
There are 2 independent parts, one for each index of `groups`. A program takes and returns all parts, laid end to end along the dimension named above; an argument that names none is the same for every part. Nothing has to cross between parts.
Inputs may be any that keep to these rules, and one draw needn't show every extreme that they name: `adapter_slot`: each slot holds exactly one adapter. `block_adapter`: every adapter is named by some block. `live_tokens`: one index of dp has all its rows live.
All inputs are finite; a program needn't handle non-finite values. No bound on the sum of `live_tokens` on one device may be relied on, other than what follows from the above.
Results may differ from a plain program's by a relative error of at most 0.02.
Values may be sent and summed in bfloat16 or wider, within the bound.
A program may use at most 64 MiB of HBM per device.

v0:
```python
import jax
import jax.numpy as jnp
from jax import lax
from jax.sharding import PartitionSpec as P

HD = 128
R = 32
REQUEST_ROWS = 128


adapter_alpha_factor = 32.0
rope_theta = 500000.0


def rope_tables(length, width):
    halfway = width // 2
    spread = rope_theta ** (-2.0 * jnp.arange(halfway, dtype=jnp.float32) / width)
    angle = jnp.arange(length, dtype=jnp.float32)[:, None] * spread[None, :]
    return (jnp.cos(angle), jnp.sin(angle))


def rotate(value_matrix, cosine, sine):
    halfway = value_matrix.shape[-1] // 2
    first = value_matrix[..., :halfway]
    second = value_matrix[..., halfway:]
    cos_grid = cosine[:, None, :]
    sin_grid = sine[:, None, :]
    return jnp.concatenate(
        [first * cos_grid - second * sin_grid, second * cos_grid + first * sin_grid], axis=-1
    )


def attention_grads(queries, keys, value_matrix, dout, allowed, group):
    request_block_count, length, heads, depth = queries.shape
    kv_heads = keys.shape[2]
    grouped_q = queries.reshape(request_block_count, length, kv_heads, group, depth)
    grouped_d = dout.reshape(request_block_count, length, kv_heads, group, depth)
    scores = jnp.einsum(
        "ntkge,nske->nkgts", grouped_q, keys, preferred_element_type=jnp.float32
    ) * depth ** (-0.5)
    scores = jnp.where(allowed[:, None, None], scores, -1e30)
    summit = jnp.max(scores, axis=-1, keepdims=True)
    expo = jnp.exp(scores - summit)
    probs = expo / jnp.sum(expo, axis=-1, keepdims=True)
    dprobs = jnp.einsum(
        "ntkge,nske->nkgts", grouped_d, value_matrix, preferred_element_type=jnp.float32
    )
    dscores = probs * (dprobs - jnp.sum(dprobs * probs, axis=-1, keepdims=True))
    dscore_b = dscores.astype(jnp.bfloat16)
    dquery = jnp.einsum(
        "nkgts,nske->ntkge", dscore_b, keys, preferred_element_type=jnp.float32
    ) * depth ** (-0.5)
    prob_b = probs.astype(jnp.bfloat16)
    dvalue = jnp.einsum("nkgts,ntkge->nske", prob_b, grouped_d, preferred_element_type=jnp.float32)
    return (dquery.reshape(request_block_count, length, heads, depth), dvalue)


def on_device(
    tokens,
    w_query,
    w_key,
    w_value,
    a_query,
    b_query,
    a_value,
    b_value,
    adapter_ranks,
    adapter_slot,
    block_adapter,
    live_tokens,
    d_heads,
):
    row_count = tokens.shape[0]
    request_block_count = row_count // REQUEST_ROWS
    local_width = a_query.shape[1]
    query_column_count = w_query.shape[1]
    value_column_count = w_key.shape[1]
    local_heads = query_column_count // HD
    local_kv = value_column_count // HD
    group = local_heads // local_kv
    dp_count = lax.axis_size("dp")
    owned = a_query.shape[0]
    adapter_count = owned * dp_count
    cosine, sine = rope_tables(REQUEST_ROWS, HD)
    column_start = lax.axis_index("tensor") * local_width
    tok_local = lax.dynamic_slice_in_dim(tokens, column_start, local_width, 1)
    full_q, full_k, full_v = (
        lax.all_gather(w_query, "dp", axis=0, tiled=True),
        lax.all_gather(w_key, "dp", axis=0, tiled=True),
        lax.all_gather(w_value, "dp", axis=0, tiled=True),
    )
    frozen_query = jnp.dot(tokens, full_q, preferred_element_type=jnp.float32)
    base_k = jnp.dot(tokens, full_k, preferred_element_type=jnp.float32)
    frozen_value = jnp.dot(tokens, full_v, preferred_element_type=jnp.float32)
    all_aq, all_bq, all_av, all_bv = (
        lax.all_gather(a_query, "dp", axis=0, tiled=True),
        lax.all_gather(b_query, "dp", axis=0, tiled=True),
        lax.all_gather(a_value, "dp", axis=0, tiled=True),
        lax.all_gather(b_value, "dp", axis=0, tiled=True),
    )
    block_ids = block_adapter[:, 0]
    slot_ids = adapter_slot[block_ids]
    rank_index_list = adapter_ranks[block_ids]
    adapter_scale = (adapter_alpha_factor / rank_index_list.astype(jnp.float32))[:, None, None]
    keep = (jnp.arange(R, dtype=jnp.int32)[None, :] < rank_index_list[:, None]).astype(jnp.float32)[
        :, None, :
    ]
    aq_sel = all_aq[slot_ids]
    av_sel = all_av[slot_ids]
    selected_query_up = all_bq[slot_ids]
    selected_value_up = all_bv[slot_ids]
    block_local = tok_local.reshape(request_block_count, REQUEST_ROWS, local_width)
    part_q = jnp.einsum("ntd,ndr->ntr", block_local, aq_sel, preferred_element_type=jnp.float32)
    part_v = jnp.einsum("ntd,ndr->ntr", block_local, av_sel, preferred_element_type=jnp.float32)
    sum_q, sum_v = lax.psum((part_q, part_v), "tensor")
    query_down_weight = (sum_q * keep).astype(jnp.bfloat16)
    value_down_weight = (sum_v * keep).astype(jnp.bfloat16)
    adapter_query_delta = jnp.einsum(
        "zwf,zfy->zwy", query_down_weight, selected_query_up, preferred_element_type=jnp.float32
    )
    complete_query = (
        frozen_query.reshape(request_block_count, REQUEST_ROWS, query_column_count)
        + adapter_scale * adapter_query_delta
    )
    queries = rotate(
        complete_query.reshape(request_block_count, REQUEST_ROWS, local_heads, HD), cosine, sine
    ).astype(jnp.bfloat16)
    keys = rotate(
        base_k.reshape(request_block_count, REQUEST_ROWS, local_kv, HD), cosine, sine
    ).astype(jnp.bfloat16)
    adapter_value_delta = jnp.einsum(
        "zwf,zfy->zwy", value_down_weight, selected_value_up, preferred_element_type=jnp.float32
    )
    value_matrix = (
        frozen_value.reshape(request_block_count, REQUEST_ROWS, value_column_count)
        + adapter_scale * adapter_value_delta
    ).astype(jnp.bfloat16)
    value_matrix = value_matrix.reshape(request_block_count, REQUEST_ROWS, local_kv, HD)
    position = jnp.arange(REQUEST_ROWS, dtype=jnp.int32)
    causal = position[None, :] <= position[:, None]
    diagonal = position[None, :] == position[:, None]
    row_index = jnp.arange(row_count, dtype=jnp.int32).reshape(request_block_count, REQUEST_ROWS)
    live = row_index < live_tokens[0]
    allowed = causal[None] & (live[:, None, :] | diagonal[None])
    dout = jnp.where(
        live[:, :, None],
        d_heads.reshape(request_block_count, REQUEST_ROWS, query_column_count),
        jnp.zeros((), jnp.bfloat16),
    )
    dquery, dvalue = attention_grads(
        queries,
        keys,
        value_matrix,
        dout.reshape(request_block_count, REQUEST_ROWS, local_heads, HD),
        allowed,
        group,
    )
    grad_q = (
        rotate(dquery, cosine, -sine)
        .reshape(request_block_count, REQUEST_ROWS, query_column_count)
        .astype(jnp.bfloat16)
    )
    grad_v = dvalue.reshape(request_block_count, REQUEST_ROWS, value_column_count).astype(
        jnp.bfloat16
    )
    up_q = adapter_scale * jnp.einsum(
        "ntr,ntc->nrc", query_down_weight, grad_q, preferred_element_type=jnp.float32
    )
    up_v = adapter_scale * jnp.einsum(
        "ntr,ntc->nrc", value_down_weight, grad_v, preferred_element_type=jnp.float32
    )
    part_back_q = adapter_scale * jnp.einsum(
        "ntc,nrc->ntr", grad_q, selected_query_up, preferred_element_type=jnp.float32
    )
    part_back_v = adapter_scale * jnp.einsum(
        "ntc,nrc->ntr", grad_v, selected_value_up, preferred_element_type=jnp.float32
    )
    whole_q, whole_v = (
        lax.psum(part_back_q.astype(jnp.bfloat16), "tensor").astype(jnp.float32),
        lax.psum(part_back_v.astype(jnp.bfloat16), "tensor").astype(jnp.float32),
    )
    back_q = (whole_q * keep).astype(jnp.bfloat16)
    back_v = (whole_v * keep).astype(jnp.bfloat16)
    low_q = jnp.einsum("ntd,ntr->ndr", block_local, back_q, preferred_element_type=jnp.float32)
    low_v = jnp.einsum("ntd,ntr->ndr", block_local, back_v, preferred_element_type=jnp.float32)
    onehot = (jnp.arange(adapter_count, dtype=jnp.int32)[:, None] == slot_ids[None, :]).astype(
        jnp.float32
    )
    placed = tuple((jnp.einsum("an,nxy->axy", onehot, item) for item in (low_q, up_q, low_v, up_v)))
    rounded = tuple((item.astype(jnp.bfloat16) for item in placed))
    arrived = (
        lax.all_to_all(rounded[0], "dp", split_axis=0, concat_axis=0, tiled=True),
        lax.all_to_all(rounded[1], "dp", split_axis=0, concat_axis=0, tiled=True),
        lax.all_to_all(rounded[2], "dp", split_axis=0, concat_axis=0, tiled=True),
        lax.all_to_all(rounded[3], "dp", split_axis=0, concat_axis=0, tiled=True),
    )
    summed = tuple(
        (
            jnp.sum(item.astype(jnp.float32).reshape((dp_count, owned) + item.shape[1:]), axis=0)
            for item in arrived
        )
    )
    grad_aq, grad_bq, grad_av, grad_bv = summed
    return (grad_aq, grad_bq, grad_av, grad_bv)


def solution(mesh):
    in_specs = (
        P(("groups", "dp"), None),
        P("dp", "tensor"),
        P("dp", "tensor"),
        P("dp", "tensor"),
        P(("groups", "dp"), "tensor", None),
        P(("groups", "dp"), None, "tensor"),
        P(("groups", "dp"), "tensor", None),
        P(("groups", "dp"), None, "tensor"),
        P("groups"),
        P(),
        P(("groups", "dp"), None),
        P(("groups", "dp")),
        P(("groups", "dp"), "tensor"),
    )
    out_specs = (
        P(("groups", "dp"), "tensor", None),
        P(("groups", "dp"), None, "tensor"),
        P(("groups", "dp"), "tensor", None),
        P(("groups", "dp"), None, "tensor"),
    )
    return jax.shard_map(
        on_device, mesh=mesh, in_specs=in_specs, out_specs=out_specs, check_vma=False
    )
```

profile of v0, /device:TPU:9, one launch (start us, length us, event | category | flops | bytes accessed | tf_op | source)
XLA Modules:
  0.0 363.5 jit_solution(496045043462790063)
XLA Ops:
  10.9 12.8 %all_gather.23 = bf16[4,1024,32]{1,2,0:T(8,128)(2,1)S(1)} all-gather(bf16[1,1024,32]{1,2,0:T(8,128)(2,1)} %param.17), channel_id=1, replica_groups=mesh['groups'=2,'dp'=4,'tensor'=4] {'dp'}, dimensions={0}, use_global_device_ids=true | all-gather | bytes 327680 | tf_op jit(solution)/shard_map/all_gather | solution.py:96
  24.3 13.8 %all_gather.26 = bf16[4,1024,32]{1,2,0:T(8,128)(2,1)S(1)} all-gather(bf16[1,1024,32]{1,2,0:T(8,128)(2,1)S(1)} %copy-done.11), channel_id=1, replica_groups=mesh['groups'=2,'dp'=4,'tensor'=4] {'dp'}, dimensions={0}, use_global_device_ids=true | all-gather | bytes 327680 | tf_op jit(solution)/shard_map/all_gather | solution.py:98
  38.6 1.3 constant_dynamic-slice_fusion
  39.9 1.1 fusion.65
  41.1 1.1 fusion.63
  44.2 11.7 %all_gather.27 = bf16[4,32,256]{2,1,0:T(8,128)(2,1)S(1)} all-gather(bf16[1,32,256]{2,1,0:T(8,128)(2,1)S(1)} %copy-done.15), channel_id=1, replica_groups=mesh['groups'=2,'dp'=4,'tensor'=4] {'dp'}, dimensions={0}, use_global_device_ids=true | all-gather | bytes 81920 | tf_op jit(solution)/shard_map/all_gather | solution.py:99
  56.5 10.8 %all_gather.24 = bf16[4,32,1024]{2,1,0:T(8,128)(2,1)S(1)} all-gather(bf16[1,32,1024]{2,1,0:T(8,128)(2,1)S(1)} %copy-done.12), channel_id=1, replica_groups=mesh['groups'=2,'dp'=4,'tensor'=4] {'dp'}, dimensions={0}, use_global_device_ids=true | all-gather | bytes 327680 | tf_op jit(solution)/shard_map/all_gather | solution.py:97
  68.7 1.5 copy.45
  72.0 4.4 %fusion.61 = f32[512,256]{1,0:T(8,128)S(1)} fusion(bf16[512,4096]{1,0:T(8,128)(2,1)} %param.13, bf16[4096,256]{1,0:T(8,128)(2,1)} %all-gather.4.cloned.1.call-done), kind=kOutput, calls=%fused_computation.101 | convolution fusion | flops 1073741824 | bytes 6815744 | tf_op jit(solution)/shard_map/dot_general | solution.py:93
  76.6 32.2 %all-gather.8.cloned.1.call-done = bf16[4096,256]{1,0:T(8,128)(2,1)} async-done(((bf16[1024,256]{1,0:T(8,128)(2,1)}), bf16[4096,256]{1,0:T(8,128)(2,1)}) %all-gather.8.cloned.1.call-update) | async-done | bytes 2097168 | tf_op jit(solution)/shard_map/all_gather | solution.py:90
  108.8 4.1 %fusion.64 = f32[512,256]{1,0:T(8,128)S(1)} fusion(bf16[512,4096]{1,0:T(8,128)(2,1)} %param.13, bf16[4096,256]{1,0:T(8,128)(2,1)} %all-gather.8.cloned.1.call-done), kind=kOutput, calls=%fused_computation.104 | convolution fusion | flops 1073741824 | bytes 6815744 | tf_op jit(solution)/shard_map/dot_general | solution.py:94
  113.0 1.2 fusion.6
  115.6 1.0 subtract_convert_fusion.2
  116.6 141.1 %all-gather.6.cloned.1.call-done = bf16[4096,1024]{1,0:T(8,128)(2,1)} async-done(((bf16[1024,1024]{1,0:T(8,128)(2,1)}), bf16[4096,1024]{1,0:T(8,128)(2,1)}) %all-gather.6.cloned.1.call-update) | async-done | bytes 8388624 | tf_op jit(solution)/shard_map/all_gather | solution.py:88
  257.7 8.3 %fusion.62 = f32[512,1024]{1,0:T(8,128)S(1)} fusion(bf16[512,4096]{1,0:T(8,128)(2,1)} %param.13, bf16[4096,1024]{1,0:T(8,128)(2,1)} %all-gather.6.cloned.1.call-done), kind=kOutput, calls=%fused_computation.102 | convolution fusion | flops 4294967296 | bytes 14680064 | tf_op jit(solution)/shard_map/dot_general | solution.py:92
  268.1 1.2 copy.44
  269.3 4.7 %fusion.58 = (f32[4,2,4,128]{3,2,1,0:T(4,128)}, f32[4,2,4,128,128]{3,4,2,1,0:T(8,128)}) fusion(pred[4,128,128]{1,2,0:T(8,128)(4,1)} %or_and_fusion, bf16[4,128,2,4,64]{4,1,3,2,0:T(8,128)(2,1)} %bitcast.100, bf16[4,128,2,4,64]{4,1,3,2,0:T(8,128)(2,1)S(1)} %bitcast.99, bf16[4,128,2,64]{3,1,2,0:T(8,128)(2,1)} %get-tuple-element.15, ...), kind=kOutput, calls=%fused_computation.100 | convolution fusion | flops 138936448 | bytes 3489792 | tf_op jit(solution)/shard_map/sub | solution.py:43
  274.1 2.2 fusion.7
  279.7 1.5 fusion.56
  281.1 1.9 copy.79
  283.1 3.2 copy.78
  286.3 2.2 subtract_convert_fusion
  289.6 1.1 fusion.8
  291.9 6.6 %all-to-all-start.3 = ((bf16[4,32,256]{2,1,0:T(8,128)(2,1)}), bf16[4,32,256]{2,1,0:T(8,128)(2,1)S(1)}, u32[]{:S(2)}, u32[]{:S(2)}) async-start(bf16[4,32,256]{2,1,0:T(8,128)(2,1)} %copy.62), calls=%async_computation.3 | async-start | bytes 131072 | tf_op jit(solution)/shard_map/all_to_all | solution.py:195
  300.2 2.1 all-to-all-done.3
  302.3 4.2 %all-to-all-start.1 = ((bf16[4,32,1024]{2,1,0:T(8,128)(2,1)}), bf16[4,32,1024]{2,1,0:T(8,128)(2,1)S(1)}, u32[]{:S(2)}, u32[]{:S(2)}) async-start(bf16[4,32,1024]{2,1,0:T(8,128)(2,1)} %copy.55), calls=%async_computation.1 | async-start | bytes 524288 | tf_op jit(solution)/shard_map/all_to_all | solution.py:193
  306.5 26.7 %all-reduce.7.cloned.1.call-done = (bf16[4,128,32]{1,2,0:T(8,128)(2,1)}, bf16[4,128,32]{1,2,0:T(8,128)(2,1)}) async-done(((bf16[4,128,32]{1,2,0:T(8,128)(2,1)}, bf16[4,128,32]{1,2,0:T(8,128)(2,1)}), (bf16[4,128,32]{1,2,0:T(8,128)(2,1)}, bf16[4,128,32]{1,2,0:T(8,128)(2,1)})) %all-reduce.7.cloned.1.call-update) | async-done | bytes 65552 | tf_op jit(solution)/shard_map/psum | solution.py:179
  333.2 1.1 fusion.35
  335.3 4.6 %all-to-all-start.2 = ((bf16[4,1024,32]{1,2,0:T(8,128)(2,1)}), bf16[4,1024,32]{1,2,0:T(8,128)(2,1)S(1)}, u32[]{:S(2)}, u32[]{:S(2)}) async-start(bf16[4,1024,32]{1,2,0:T(8,128)(2,1)} %copy.59), calls=%async_computation.2 | async-start | bytes 524288 | tf_op jit(solution)/shard_map/all_to_all | solution.py:194
  341.3 4.0 %all-to-all-done.2 = bf16[4,1024,32]{1,2,0:T(8,128)(2,1)S(1)} async-done(((bf16[4,1024,32]{1,2,0:T(8,128)(2,1)}), bf16[4,1024,32]{1,2,0:T(8,128)(2,1)S(1)}, u32[]{:S(2)}, u32[]{:S(2)}) %all-to-all-start.2) | async-done | bytes 262176 | tf_op jit(solution)/shard_map/all_to_all | solution.py:194
  345.3 5.0 %all-to-all-start = ((bf16[4,1024,32]{1,2,0:T(8,128)(2,1)}), bf16[4,1024,32]{1,2,0:T(8,128)(2,1)S(1)}, u32[]{:S(2)}, u32[]{:S(2)}) async-start(bf16[4,1024,32]{1,2,0:T(8,128)(2,1)} %copy.53), calls=%async_computation | async-start | bytes 524288 | tf_op jit(solution)/shard_map/all_to_all | solution.py:192
  352.4 3.3 all-to-all-done
  (98 shorter events, 25.1 us)
Async XLA Ops:
  8.0 2.2 copy-start
  8.0 16.3 %copy-start.11 = (bf16[1,1024,32]{1,2,0:T(8,128)(2,1)S(1)}, bf16[1,1024,32]{1,2,0:T(8,128)(2,1)}, u32[]{:S(2)}) copy-start(bf16[1,1024,32]{1,2,0:T(8,128)(2,1)} %param.19) | copy-start | bytes 196612
  8.0 63.9 %all-gather.4.cloned.1.call-start = ((), (), s32[]{:S(2)}) async-start(), calls=%async_computation.4 | async-start | bytes 2621440 | tf_op jit(solution)/shard_map/all_gather | solution.py:89
  8.8 100.1 %all-gather.8.cloned.1.call-start = ((), (), s32[]{:S(2)}) async-start(), calls=%async_computation.6 | async-start | bytes 2621440 | tf_op jit(solution)/shard_map/all_gather | solution.py:90
  9.5 103.5 %all-reduce.5.cloned.1.call-start = ((), (), s32[]{:S(2)}) async-start(), calls=%async_computation.7 | async-start | bytes 262144 | tf_op jit(solution)/shard_map/psum | solution.py:115
  10.9 27.8 %copy-start.16 = (s32[4]{0:T(128)}, s32[4]{0:T(128)S(1)}, u32[]{:S(2)}) copy-start(s32[4]{0:T(128)S(1)} %gather_fusion) | copy-start | bytes 52
  41.0 2.5 copy-start.1
  41.0 3.2 copy-start.15
  41.0 15.5 %copy-start.12 = (bf16[1,32,1024]{2,1,0:T(8,128)(2,1)S(1)}, bf16[1,32,1024]{2,1,0:T(8,128)(2,1)}, u32[]{:S(2)}) copy-start(bf16[1,32,1024]{2,1,0:T(8,128)(2,1)} %param.18) | copy-start | bytes 196612
  42.2 25.8 %copy-start.2 = (bf16[512,1024]{1,0:T(8,128)(2,1)S(1)}, bf16[512,1024]{1,0:T(8,128)(2,1)}, u32[]{:S(2)}) copy-start(bf16[512,1024]{1,0:T(8,128)(2,1)} %param.25) | copy-start | bytes 3145732
  42.2 215.5 %all-gather.6.cloned.1.call-start = ((), (), s32[]{:S(2)}) async-start(), calls=%async_computation.5 | async-start | bytes 10485760 | tf_op jit(solution)/shard_map/all_gather | solution.py:88
  116.6 149.4 %copy-start.4 = (f32[4,128,32]{1,2,0:T(8,128)S(1)}, f32[4,128,32]{1,2,0:T(8,128)}, u32[]{:S(2)}) copy-start(f32[4,128,32]{1,2,0:T(8,128)} %get-tuple-element.5) | copy-start | bytes 196612
  269.3 4.7 %copy-start.3 = (bf16[4,128,2,4,128]{1,4,3,2,0:T(8,128)(2,1)S(1)}, bf16[4,128,2,4,128]{1,4,3,2,0:T(8,128)(2,1)}, u32[]{:S(2)}) copy-start(bf16[4,128,2,4,128]{1,4,3,2,0:T(8,128)(2,1)} %copy.45) | copy-start | bytes 3145732
  274.1 3.0 copy-start.8
  274.1 3.9 %copy-start.7 = (bf16[4,128,2,128]{3,2,1,0:T(2,128)(2,1)S(1)}, bf16[4,128,2,128]{3,2,1,0:T(2,128)(2,1)}, u32[]{:S(2)}) copy-start(bf16[4,128,2,128]{3,2,1,0:T(2,128)(2,1)} %reshape.212) | copy-start | bytes 786436
  274.1 3.9 %copy-start.18 = (f32[4,2,4,128,128]{3,4,2,1,0:T(8,128)S(1)}, f32[4,2,4,128,128]{3,4,2,1,0:T(8,128)}, u32[]{:S(2)}) copy-start(f32[4,2,4,128,128]{3,4,2,1,0:T(8,128)} %get-tuple-element.22) | copy-start | bytes 6291460
  274.1 3.9 %copy-start.19 = (f32[4,2,4,128]{3,2,1,0:T(4,128)S(1)}, f32[4,2,4,128]{3,2,1,0:T(4,128)}, u32[]{:S(2)}) copy-start(f32[4,2,4,128]{3,2,1,0:T(4,128)} %get-tuple-element.21) | copy-start | bytes 49156
  278.0 1.0 copy-start.9
  278.0 1.0 copy-start.10
  283.1 3.2 copy-start.6
  289.1 1.6 copy-start.5
  289.1 1.9 copy-start.13
  289.1 1.9 copy-start.17
  291.9 10.4 %all-to-all-start.3 = ((bf16[4,32,256]{2,1,0:T(8,128)(2,1)}), bf16[4,32,256]{2,1,0:T(8,128)(2,1)S(1)}, u32[]{:S(2)}, u32[]{:S(2)}) async-start(bf16[4,32,256]{2,1,0:T(8,128)(2,1)} %copy.62), calls=%async_computation.3 | async-start | bytes 131072 | tf_op jit(solution)/shard_map/all_to_all | solution.py:195
  298.5 34.6 %all-reduce.7.cloned.1.call-start = ((), (), s32[]{:S(2)}) async-start(), calls=%async_computation.8 | async-start | bytes 131072 | tf_op jit(solution)/shard_map/psum | solution.py:179
  302.3 33.1 %all-to-all-start.1 = ((bf16[4,32,1024]{2,1,0:T(8,128)(2,1)}), bf16[4,32,1024]{2,1,0:T(8,128)(2,1)S(1)}, u32[]{:S(2)}, u32[]{:S(2)}) async-start(bf16[4,32,1024]{2,1,0:T(8,128)(2,1)} %copy.55), calls=%async_computation.1 | async-start | bytes 524288 | tf_op jit(solution)/shard_map/all_to_all | solution.py:193
  333.1 6.8 %copy-start.14 = (bf16[4,128,32]{1,2,0:T(8,128)(2,1)S(1)}, bf16[4,128,32]{1,2,0:T(8,128)(2,1)}, u32[]{:S(2)}) copy-start(bf16[4,128,32]{1,2,0:T(8,128)(2,1)} %get-tuple-element.6) | copy-start | bytes 98308
  335.3 10.0 %all-to-all-start.2 = ((bf16[4,1024,32]{1,2,0:T(8,128)(2,1)}), bf16[4,1024,32]{1,2,0:T(8,128)(2,1)S(1)}, u32[]{:S(2)}, u32[]{:S(2)}) async-start(bf16[4,1024,32]{1,2,0:T(8,128)(2,1)} %copy.59), calls=%async_computation.2 | async-start | bytes 524288 | tf_op jit(solution)/shard_map/all_to_all | solution.py:194
  345.3 10.4 %all-to-all-start = ((bf16[4,1024,32]{1,2,0:T(8,128)(2,1)}), bf16[4,1024,32]{1,2,0:T(8,128)(2,1)S(1)}, u32[]{:S(2)}, u32[]{:S(2)}) async-start(bf16[4,1024,32]{1,2,0:T(8,128)(2,1)} %copy.53), calls=%async_computation | async-start | bytes 524288 | tf_op jit(solution)/shard_map/all_to_all | solution.py:192
Sparse Core Ops, SparseCore 0:
  10.4 51.1 all-gather.3
  63.1 45.6 all-gather.7
  110.4 147.2 all-gather.5
Sparse Core Ops, SparseCore 1:
  42.3 37.1 all-reduce.4
  301.9 31.2 all-reduce.6
where the time goes:
time: 369 us; the launch traced here: 364 us
  waiting for transfers between devices  212 us (57%)
  blocking collectives  49.2 us (13%)
  matrix products  34.4 us (9%)
  local copies, waits for them, and re-layouts  21.3 us (6%)
  starting transfers between devices  20.6 us (6%)
  between operations  16.2 us (4%)
  other arithmetic  9.72 us (3%)
    all_gather x1, waiting for transfers between devices, on_device(): lax.all_gather(w_query, 'dp', axis=0, tiled=True)  141 us
    all_gather x1, waiting for transfers between devices, on_device(): lax.all_gather(w_value, 'dp', axis=0, tiled=True)  32.2 us
    psum x1, waiting for transfers between devices, on_device(): lax.psum(part_back_q.astype(jnp.bfloat16), 'tensor').astype(jnp.float32)  26.7 us
    all_gather x1, blocking collectives, on_device(): lax.all_gather(a_value, 'dp', axis=0, tiled=True)  13.8 us
    all_gather x1, blocking collectives, on_device(): lax.all_gather(a_query, 'dp', axis=0, tiled=True)  12.8 us
    all_gather x1, blocking collectives, on_device(): lax.all_gather(b_value, 'dp', axis=0, tiled=True)  11.7 us
    all_gather x1, blocking collectives, on_device(): lax.all_gather(b_query, 'dp', axis=0, tiled=True)  10.8 us
    dot_general x1, matrix products, on_device(): frozen_query = jnp.dot(tokens, full_q, preferred_element_type=jnp.float32)  8.32 us
  transfers between devices with their start and end apart: 9, of which 6 were waited for; matrix products, arithmetic and copies ran while one was open for 8% of the time, Pallas kernels for 0%

commit v1 on v0

v1 whole, which is shorter than its diff:
```python
import functools

import jax
import jax.numpy as jnp
from jax import lax
from jax.experimental import pallas as pl
from jax.experimental.pallas import tpu as pltpu
from jax.sharding import PartitionSpec as P

HD = 128
R = 32
REQUEST_ROWS = 128
MESH = pl.DeviceIdType.MESH


adapter_alpha_factor = 32.0
rope_theta = 500000.0


def rope_tables(length, width):
    halfway = width // 2
    spread = rope_theta ** (-2.0 * jnp.arange(halfway, dtype=jnp.float32) / width)
    angle = jnp.arange(length, dtype=jnp.float32)[:, None] * spread[None, :]
    return (jnp.cos(angle), jnp.sin(angle))


def rotate(value_matrix, cosine, sine):
    halfway = value_matrix.shape[-1] // 2
    first = value_matrix[..., :halfway]
    second = value_matrix[..., halfway:]
    cos_grid = cosine[:, None, :]
    sin_grid = sine[:, None, :]
    return jnp.concatenate(
        [first * cos_grid - second * sin_grid, second * cos_grid + first * sin_grid], axis=-1
    )


def attention_grads(queries, keys, value_matrix, dout, allowed, group):
    request_block_count, length, heads, depth = queries.shape
    kv_heads = keys.shape[2]
    grouped_q = queries.reshape(request_block_count, length, kv_heads, group, depth)
    grouped_d = dout.reshape(request_block_count, length, kv_heads, group, depth)
    scores = jnp.einsum(
        "ntkge,nske->nkgts", grouped_q, keys, preferred_element_type=jnp.float32
    ) * depth ** (-0.5)
    scores = jnp.where(allowed[:, None, None], scores, -1e30)
    summit = jnp.max(scores, axis=-1, keepdims=True)
    expo = jnp.exp(scores - summit)
    probs = expo / jnp.sum(expo, axis=-1, keepdims=True)
    dprobs = jnp.einsum(
        "ntkge,nske->nkgts", grouped_d, value_matrix, preferred_element_type=jnp.float32
    )
    dscores = probs * (dprobs - jnp.sum(dprobs * probs, axis=-1, keepdims=True))
    dscore_b = dscores.astype(jnp.bfloat16)
    dquery = jnp.einsum(
        "nkgts,nske->ntkge", dscore_b, keys, preferred_element_type=jnp.float32
    ) * depth ** (-0.5)
    prob_b = probs.astype(jnp.bfloat16)
    dvalue = jnp.einsum("nkgts,ntkge->nske", prob_b, grouped_d, preferred_element_type=jnp.float32)
    return (dquery.reshape(request_block_count, length, heads, depth), dvalue)


def greet(axes):
    barrier = pltpu.get_barrier_semaphore()
    total = 0
    for axis in axes:
        size = lax.axis_size(axis)
        me = lax.axis_index(axis)

        @pl.loop(1, size)
        def _(j):
            pl.semaphore_signal(
                barrier, inc=1, device_id={axis: lax.rem(me + j, size)}, device_id_type=MESH
            )

        total += size - 1
    pl.semaphore_wait(barrier, total)


def project_kernel(
    pieces,
    slot_ref,
    rank_ref,
    scale_ref,
    x_hbm,
    wq_hbm,
    wk_hbm,
    wv_hbm,
    down_ref,
    bq_ref,
    bv_ref,
    acc_ref,
    u_ref,
    bq_sel_ref,
    bv_sel_ref,
    x_ref,
    w_all,
    down_all,
    bq_all,
    bv_all,
    parts,
    local_sem,
    z_send,
    z_recv,
    y_send,
    y_recv,
    f_send,
    f_recv,
    u_send,
    u_recv,
):
    n = lax.axis_size("dp")
    ng = lax.axis_size("groups")
    nt = lax.axis_size("tensor")
    me = lax.axis_index("dp")
    g = lax.axis_index("groups")
    t = lax.axis_index("tensor")
    depth = w_all.shape[1]
    cols = w_all.shape[2]
    qcols = wq_hbm.shape[1]
    kcols = wk_hbm.shape[1]
    half = depth // ng
    step = half // pieces
    rows = x_ref.shape[0]
    width = down_ref.shape[1]
    block_count = rows // REQUEST_ROWS

    x_copy = pltpu.make_async_copy(x_hbm, x_ref, local_sem.at[0])
    w_copies = [
        pltpu.make_async_copy(src, w_all.at[me, :, pl.ds(at, src.shape[1])], local_sem.at[1 + i])
        for i, (src, at) in enumerate(((wq_hbm, 0), (wk_hbm, qcols), (wv_hbm, qcols + kcols)))
    ]
    f_copies = [
        pltpu.make_async_copy(src, dst.at[me], local_sem.at[4 + i])
        for i, (src, dst) in enumerate(((down_ref, down_all), (bq_ref, bq_all), (bv_ref, bv_all)))
    ]
    for copy in w_copies + f_copies + [x_copy]:
        copy.start()
    greet(("dp", "tensor", "groups"))

    def factor_copies(j, arriving):
        peer = lax.rem(me + n - j, n) if arriving else lax.rem(me + j, n)
        at = peer if arriving else me
        return [
            pltpu.make_async_remote_copy(
                src_ref=src,
                dst_ref=dst.at[at],
                send_sem=f_send.at[i, j],
                recv_sem=f_recv.at[i, j],
                device_id={"dp": peer},
                device_id_type=MESH,
            )
            for i, (src, dst) in enumerate(
                ((down_ref, down_all), (bq_ref, bq_all), (bv_ref, bv_all))
            )
        ]

    @pl.loop(1, n)
    def _(j):
        for copy in factor_copies(j, False):
            copy.start()

    def piece(s, owner, p):
        return w_all.at[s, pl.ds(pl.multiple_of(owner * half + p * step, step), step), :]

    def z_copy(s, p, way):
        target = jnp.clip(me + (1 if way == 0 else -1), 0, n - 1)
        return pltpu.make_async_remote_copy(
            src_ref=piece(s, g, p),
            dst_ref=piece(s, g, p),
            send_sem=z_send.at[way, s, p],
            recv_sem=z_recv.at[s, p],
            device_id={"dp": target},
            device_id_type=MESH,
        )

    def y_copy(s, p, j, arriving):
        owner = lax.rem(g + ng - j, ng) if arriving else g
        return pltpu.make_async_remote_copy(
            src_ref=piece(s, owner, p),
            dst_ref=piece(s, owner, p),
            send_sem=y_send.at[j, s, p],
            recv_sem=y_recv.at[j, s, p],
            device_id={"groups": lax.rem(g + j, ng)},
            device_id_type=MESH,
        )

    for copy in w_copies:
        copy.wait()

    @pl.when(me < n - 1)
    def _():
        for p in range(pieces):
            z_copy(me, p, 0).start()

    @pl.when(me > 0)
    def _():
        for p in range(pieces):
            z_copy(me, p, 1).start()

    tile = 256 if cols % 256 == 0 else 128

    def multiply(s):
        ks = pl.ds(pl.multiple_of(s * depth, 128), depth)

        @pl.loop(0, cols // tile)
        def _(c):
            cs = pl.ds(pl.multiple_of(c * tile, tile), tile)
            acc_ref[:, cs] += jnp.dot(
                x_ref[:, ks], w_all[s, :, cs], preferred_element_type=jnp.float32
            )

    x_copy.wait()
    for copy in f_copies:
        copy.wait()
    acc_ref[...] = jnp.zeros_like(acc_ref)

    @pl.loop(1, n)
    def _(j):
        for copy in factor_copies(j, True):
            copy.wait_recv()

    mine = pl.ds(pl.multiple_of(t * width, 128), width)
    for b in range(block_count):
        span = pl.ds(b * REQUEST_ROWS, REQUEST_ROWS)
        slot = slot_ref[b]
        parts[t, span, :] = lax.dot_general(
            x_ref[span, mine],
            down_all[slot],
            (((1,), (1,)), ((), ())),
            preferred_element_type=jnp.float32,
        )
        bq_sel_ref[b] = bq_all[slot]
        bv_sel_ref[b] = bv_all[slot]

    multiply(me)

    def part_copy(j, arriving):
        peer = lax.rem(t + nt - j, nt) if arriving else lax.rem(t + j, nt)
        at = peer if arriving else t
        return pltpu.make_async_remote_copy(
            src_ref=parts.at[at],
            dst_ref=parts.at[at],
            send_sem=u_send.at[j],
            recv_sem=u_recv.at[j],
            device_id={"tensor": peer},
            device_id_type=MESH,
        )

    for j in range(1, nt):
        part_copy(j, False).start()

    def finish(s, valid):
        @pl.when(valid)
        def _():
            for p in range(pieces):
                for j in range(1, ng):
                    y_copy(s, p, j, True).wait_recv()
            multiply(s)

    def both(d):
        for p in range(pieces):
            for way in (0, 1):
                s = me - d if way == 0 else me + d
                valid = (s >= 0) if way == 0 else (s < n)
                onward = (me < n - 1) if way == 0 else (me > 0)

                @pl.when(valid)
                def _():
                    z_copy(s, p, way).wait_recv()

                    @pl.when(onward)
                    def _():
                        z_copy(s, p, way).start()

                    for j in range(1, ng):
                        y_copy(s, p, j, False).start()

    both(1)

    for j in range(1, nt):
        part_copy(j, True).wait_recv()
    for b in range(block_count):
        span = pl.ds(b * REQUEST_ROWS, REQUEST_ROWS)
        rank = rank_ref[b]
        total = parts[0, span, :]
        for j in range(1, nt):
            total = total + parts[j, span, :]
        lane = lax.broadcasted_iota(jnp.int32, total.shape, 1)
        lane = jnp.where(lane >= R, lane - R, lane)
        u = jnp.where(lane < rank, total, 0.0).astype(jnp.bfloat16)
        u_ref[span, :] = u
        acc_ref[span, :qcols] += scale_ref[b] * jnp.dot(
            u[:, :R], bq_sel_ref[b], preferred_element_type=jnp.float32
        )
        acc_ref[span, qcols + kcols :] += scale_ref[b] * jnp.dot(
            u[:, R:], bv_sel_ref[b], preferred_element_type=jnp.float32
        )

    @pl.loop(2, n + 1)
    def _(d):
        @pl.when(d < n)
        def _():
            both(d)

        finish(me - d + 1, me - d + 1 >= 0)
        finish(me + d - 1, me + d - 1 < n)

    @pl.loop(1, n)
    def _(j):
        for copy in factor_copies(j, False):
            copy.wait_send()

    for j in range(1, nt):
        part_copy(j, False).wait_send()

    @pl.loop(0, n)
    def _(s):
        for p in range(pieces):

            @pl.when((s <= me) & (me < n - 1))
            def _():
                z_copy(s, p, 0).wait_send()

            @pl.when((s >= me) & (me > 0))
            def _():
                z_copy(s, p, 1).wait_send()

            @pl.when(s != me)
            def _():
                for j in range(1, ng):
                    y_copy(s, p, j, False).wait_send()


def project(tokens, w_query, w_key, w_value, down, b_query, b_value, slots, ranks, scales):
    n, ng, nt = lax.axis_size("dp"), lax.axis_size("groups"), lax.axis_size("tensor")
    rows = tokens.shape[0]
    depth, qcols = w_query.shape
    kcols = w_key.shape[1]
    cols = qcols + 2 * kcols
    half = depth // ng
    pieces = max(1, half // 128)
    blocks = rows // REQUEST_ROWS
    smem = pl.BlockSpec(memory_space=pltpu.SMEM)
    vmem = pl.BlockSpec(memory_space=pltpu.VMEM)
    hbm = pl.BlockSpec(memory_space=pltpu.HBM)
    dma = pltpu.SemaphoreType.DMA
    return pl.pallas_call(
        functools.partial(project_kernel, pieces),
        out_shape=(
            jax.ShapeDtypeStruct((rows, cols), jnp.float32),
            jax.ShapeDtypeStruct((rows, 2 * R), jnp.bfloat16),
            jax.ShapeDtypeStruct((blocks, R, qcols), jnp.bfloat16),
            jax.ShapeDtypeStruct((blocks, R, kcols), jnp.bfloat16),
        ),
        in_specs=[smem] * 3 + [hbm] * 4 + [vmem] * 3,
        out_specs=(vmem,) * 4,
        scratch_shapes=[
            pltpu.VMEM(tokens.shape, jnp.bfloat16),
            pltpu.VMEM((n, depth, cols), jnp.bfloat16),
            pltpu.VMEM((n,) + down.shape, jnp.bfloat16),
            pltpu.VMEM((n,) + b_query.shape, jnp.bfloat16),
            pltpu.VMEM((n,) + b_value.shape, jnp.bfloat16),
            pltpu.VMEM((nt, rows, 2 * R), jnp.float32),
            dma((7,)),
            dma((2, n, pieces)),
            dma((n, pieces)),
            dma((ng, n, pieces)),
            dma((ng, n, pieces)),
            dma((3, n)),
            dma((3, n)),
            dma((nt,)),
            dma((nt,)),
        ],
        compiler_params=pltpu.CompilerParams(
            collective_id=0, has_side_effects=True, vmem_limit_bytes=60 * 1024 * 1024
        ),
        name="project",
    )(slots, ranks, scales, tokens, w_query, w_key, w_value, down, b_query, b_value)


def reduce_kernel(
    x_ref,
    mask_ref,
    keep_ref,
    part_ref,
    upq_ref,
    upv_ref,
    low_out,
    upq_out,
    upv_out,
    backs,
    low_send,
    low_got,
    upq_got,
    upv_got,
    b_send,
    b_recv,
    a_send,
    a_recv,
):
    n, nt = lax.axis_size("dp"), lax.axis_size("tensor")
    me, t = lax.axis_index("dp"), lax.axis_index("tensor")
    greet(("dp", "tensor"))

    def back_copy(j, arriving):
        peer = lax.rem(t + nt - j, nt) if arriving else lax.rem(t + j, nt)
        at = peer if arriving else t
        return pltpu.make_async_remote_copy(
            src_ref=part_ref,
            dst_ref=backs.at[at],
            send_sem=b_send.at[j],
            recv_sem=b_recv.at[j],
            device_id={"tensor": peer},
            device_id_type=MESH,
        )

    def grad_copy(i, src, dst, j, arriving):
        peer = lax.rem(me + n - j, n) if arriving else lax.rem(me + j, n)
        at = peer if arriving else me
        return pltpu.make_async_remote_copy(
            src_ref=src.at[peer],
            dst_ref=dst.at[at],
            send_sem=a_send.at[i, j],
            recv_sem=a_recv.at[i, j],
            device_id={"dp": peer},
            device_id_type=MESH,
        )

    trio = ((0, upq_ref, upq_got), (1, upv_ref, upv_got), (2, low_send, low_got))
    for j in range(1, nt):
        back_copy(j, False).start()

    @pl.loop(1, n)
    def _(j):
        for i, src, dst in trio[:2]:
            grad_copy(i, src, dst, j, False).start()

    backs[t] = part_ref[...]
    for j in range(1, nt):
        back_copy(j, True).wait_recv()
    total = backs[0].astype(jnp.float32)
    for j in range(1, nt):
        total = total + backs[j].astype(jnp.float32)
    back = (total * keep_ref[...]).astype(jnp.bfloat16)

    @pl.loop(1, n + 1)
    def _(j):
        a = lax.rem(me + j, n)
        chosen = (mask_ref[a] * back).astype(jnp.bfloat16)
        low_send[a] = lax.dot_general(
            chosen, x_ref[...], (((0,), (0,)), ((), ())), preferred_element_type=jnp.float32
        ).astype(jnp.bfloat16)

        @pl.when(j < n)
        def _():
            grad_copy(2, low_send, low_got, j, False).start()

    low_got[me] = low_send[me]
    upq_got[me] = upq_ref[me]
    upv_got[me] = upv_ref[me]

    for i, src, dst in trio:

        @pl.loop(1, n)
        def _(j):
            grad_copy(i, src, dst, j, True).wait_recv()

    for got, out in ((low_got, low_out), (upq_got, upq_out), (upv_got, upv_out)):
        out[...] = jnp.zeros_like(out)

        @pl.loop(0, n)
        def _(s):
            out[...] += got[s].astype(jnp.float32)

    for j in range(1, nt):
        back_copy(j, False).wait_send()

    for i, src, dst in trio:

        @pl.loop(1, n)
        def _(j):
            grad_copy(i, src, dst, j, False).wait_send()


def reduce_grads(x_local, mask, keep, part, up_q, up_v):
    n, nt = lax.axis_size("dp"), lax.axis_size("tensor")
    rows, width = x_local.shape
    vmem = pl.BlockSpec(memory_space=pltpu.VMEM)
    dma = pltpu.SemaphoreType.DMA
    low_shape = (n, 2 * R, width)
    return pl.pallas_call(
        reduce_kernel,
        out_shape=(
            jax.ShapeDtypeStruct(low_shape[1:], jnp.float32),
            jax.ShapeDtypeStruct(up_q.shape[1:], jnp.float32),
            jax.ShapeDtypeStruct(up_v.shape[1:], jnp.float32),
        ),
        in_specs=[vmem] * 6,
        out_specs=(vmem,) * 3,
        scratch_shapes=[
            pltpu.VMEM((nt,) + part.shape, jnp.bfloat16),
            pltpu.VMEM(low_shape, jnp.bfloat16),
            pltpu.VMEM(low_shape, jnp.bfloat16),
            pltpu.VMEM(up_q.shape, jnp.bfloat16),
            pltpu.VMEM(up_v.shape, jnp.bfloat16),
            dma((nt,)),
            dma((nt,)),
            dma((3, n)),
            dma((3, n)),
        ],
        compiler_params=pltpu.CompilerParams(
            collective_id=1, has_side_effects=True, vmem_limit_bytes=60 * 1024 * 1024
        ),
        name="reduce_grads",
    )(x_local, mask, keep, part, up_q, up_v)


def on_device(
    tokens,
    w_query,
    w_key,
    w_value,
    a_query,
    b_query,
    a_value,
    b_value,
    adapter_ranks,
    adapter_slot,
    block_adapter,
    live_tokens,
    d_heads,
):
    row_count = tokens.shape[0]
    request_block_count = row_count // REQUEST_ROWS
    local_width = a_query.shape[1]
    query_column_count = w_query.shape[1]
    value_column_count = w_key.shape[1]
    local_heads = query_column_count // HD
    local_kv = value_column_count // HD
    group = local_heads // local_kv
    dp_count = lax.axis_size("dp")
    owned = a_query.shape[0]
    adapter_count = owned * dp_count
    cosine, sine = rope_tables(REQUEST_ROWS, HD)
    column_start = lax.axis_index("tensor") * local_width
    tok_local = lax.dynamic_slice_in_dim(tokens, column_start, local_width, 1)
    block_ids = block_adapter[:, 0]
    slot_ids = adapter_slot[block_ids]
    rank_index_list = adapter_ranks[block_ids]
    scales = adapter_alpha_factor / rank_index_list.astype(jnp.float32)
    adapter_scale = scales[:, None, None]
    keep = (jnp.arange(R, dtype=jnp.int32)[None, :] < rank_index_list[:, None]).astype(jnp.float32)
    down = jnp.concatenate([a_query[0].T, a_value[0].T], axis=0)
    full, low_rank, selected_query_up, selected_value_up = project(
        tokens, w_query, w_key, w_value, down, b_query[0], b_value[0],
        slot_ids, rank_index_list, scales,
    )
    shape3 = (request_block_count, REQUEST_ROWS, -1)
    query_down_weight = low_rank[:, :R].reshape(shape3)
    value_down_weight = low_rank[:, R:].reshape(shape3)
    queries = rotate(
        full[:, :query_column_count].reshape(request_block_count, REQUEST_ROWS, local_heads, HD),
        cosine, sine,
    ).astype(jnp.bfloat16)
    keys = rotate(
        full[:, query_column_count : query_column_count + value_column_count].reshape(
            request_block_count, REQUEST_ROWS, local_kv, HD
        ),
        cosine, sine,
    ).astype(jnp.bfloat16)
    value_matrix = full[:, query_column_count + value_column_count :].astype(jnp.bfloat16)
    value_matrix = value_matrix.reshape(request_block_count, REQUEST_ROWS, local_kv, HD)
    position = jnp.arange(REQUEST_ROWS, dtype=jnp.int32)
    causal = position[None, :] <= position[:, None]
    diagonal = position[None, :] == position[:, None]
    row_index = jnp.arange(row_count, dtype=jnp.int32).reshape(request_block_count, REQUEST_ROWS)
    live = row_index < live_tokens[0]
    allowed = causal[None] & (live[:, None, :] | diagonal[None])
    dout = jnp.where(
        live[:, :, None],
        d_heads.reshape(request_block_count, REQUEST_ROWS, query_column_count),
        jnp.zeros((), jnp.bfloat16),
    )
    dquery, dvalue = attention_grads(
        queries,
        keys,
        value_matrix,
        dout.reshape(request_block_count, REQUEST_ROWS, local_heads, HD),
        allowed,
        group,
    )
    grad_q = (
        rotate(dquery, cosine, -sine)
        .reshape(request_block_count, REQUEST_ROWS, query_column_count)
        .astype(jnp.bfloat16)
    )
    grad_v = dvalue.reshape(request_block_count, REQUEST_ROWS, value_column_count).astype(
        jnp.bfloat16
    )
    up_q = adapter_scale * jnp.einsum(
        "ntr,ntc->nrc", query_down_weight, grad_q, preferred_element_type=jnp.float32
    )
    up_v = adapter_scale * jnp.einsum(
        "ntr,ntc->nrc", value_down_weight, grad_v, preferred_element_type=jnp.float32
    )
    part_back_q = adapter_scale * jnp.einsum(
        "ntc,nrc->ntr", grad_q, selected_query_up, preferred_element_type=jnp.float32
    )
    part_back_v = adapter_scale * jnp.einsum(
        "ntc,nrc->ntr", grad_v, selected_value_up, preferred_element_type=jnp.float32
    )
    part_back = jnp.concatenate([part_back_q, part_back_v], axis=-1)
    part_back = part_back.reshape(row_count, 2 * R).astype(jnp.bfloat16)
    chosen = jnp.arange(adapter_count, dtype=jnp.int32)[:, None] == slot_ids[None, :]
    onehot = chosen.astype(jnp.float32)
    placed_q, placed_v = (
        jnp.einsum("an,nxy->axy", onehot, item).astype(jnp.bfloat16) for item in (up_q, up_v)
    )
    row_mask = jnp.broadcast_to(
        chosen[:, :, None, None], (adapter_count, request_block_count, REQUEST_ROWS, 2 * R)
    ).reshape(adapter_count, row_count, 2 * R).astype(jnp.bfloat16)
    row_keep = jnp.broadcast_to(
        jnp.concatenate([keep, keep], axis=-1)[:, None, :],
        (request_block_count, REQUEST_ROWS, 2 * R),
    ).reshape(row_count, 2 * R)
    low, grad_bq, grad_bv = reduce_grads(
        tok_local, row_mask, row_keep, part_back, placed_q, placed_v
    )
    return (low[:R].T[None], grad_bq[None], low[R:].T[None], grad_bv[None])


def solution(mesh):
    in_specs = (
        P(("groups", "dp"), None),
        P("dp", "tensor"),
        P("dp", "tensor"),
        P("dp", "tensor"),
        P(("groups", "dp"), "tensor", None),
        P(("groups", "dp"), None, "tensor"),
        P(("groups", "dp"), "tensor", None),
        P(("groups", "dp"), None, "tensor"),
        P("groups"),
        P(),
        P(("groups", "dp"), None),
        P(("groups", "dp")),
        P(("groups", "dp"), "tensor"),
    )
    out_specs = (
        P(("groups", "dp"), "tensor", None),
        P(("groups", "dp"), None, "tensor"),
        P(("groups", "dp"), "tensor", None),
        P(("groups", "dp"), None, "tensor"),
    )
    return jax.shard_map(
        on_device, mesh=mesh, in_specs=in_specs, out_specs=out_specs, check_vma=False
    )
```

time: 369 us -> 214 us (0.58); the launches traced: 364 us -> 214 us
  waiting for transfers between devices: 212 us -> 0 us
  Pallas kernels: 0 us -> 164 us
  blocking collectives: 49.2 us -> 0 us
  matrix products: 34.4 us -> 10.2 us
  starting transfers between devices: 20.6 us -> 0 us
  between operations: 16.2 us -> 1.61 us
  local copies, waits for them, and re-layouts: 21.3 us -> 29 us
    all_gather x3 -> x0, waiting for transfers between devices: 173 us -> none  [the longest x1 141 us: on_device(): lax.all_gather(w_query, 'dp', axis=0, tiled=True)]
    pallas_call x0 -> x2, Pallas kernels: none -> 164 us  [the longest x1 134 us: project(): pl.pallas_call(functools.partial(project_kernel, pieces), out_shape=(jax....]
    all_gather x4 -> x0, blocking collectives: 49.2 us -> none  [the longest x1 13.8 us: on_device(): lax.all_gather(a_value, 'dp', axis=0, tiled=True)]
    psum x2 -> x0, waiting for transfers between devices: 26.7 us -> none  [the longest x1 26.7 us: on_device(): lax.psum(part_back_q.astype(jnp.bfloat16), 'tensor').astype(jnp.float32)]
    dot_general x13 -> x2, matrix products: 23.3 us -> 0.7 us  [on_device(): jnp.einsum('an,nxy->axy', onehot, item).astype(jnp.bfloat16)]
    all_to_all x4 -> x0, starting transfers between devices: 20.4 us -> none  [the longest x1 6.61 us: on_device(): lax.all_to_all(rounded[3], 'dp', split_axis=0, concat_axis=0, tiled=True)]
    all_to_all x4 -> x0, waiting for transfers between devices: 9.44 us -> none  [the longest x1 3.98 us: on_device(): lax.all_to_all(rounded[2], 'dp', split_axis=0, concat_axis=0, tiled=True)]
    unnamed x43 -> x40, local copies, waits for them, and re-layouts: 6.22 us -> 9.69 us
  transfers between devices with their start and end apart: 9 -> 0, of which waited for: 6 -> 0; matrix products, arithmetic and copies ran while one was open for 8% -> 0% of each run, Pallas kernels for 0% -> 0%
where the time goes in v1:
time: 214 us
  Pallas kernels  164 us (77%)
  local copies, waits for them, and re-layouts  29 us (14%)
  matrix products  10.2 us (5%)
  other arithmetic  9.1 us (4%)
    pallas_call x1, Pallas kernels, project(): pl.pallas_call(functools.partial(project_kernel, pieces), out_shape=(jax....  134 us
    pallas_call x1, Pallas kernels, reduce_grads(): pl.pallas_call(reduce_kernel, out_shape=(jax.ShapeDtypeStruct(low_shape[1...  29.9 us
    unnamed x40, local copies, waits for them, and re-layouts  9.69 us
    sub x1, matrix products, attention_grads(): expo = jnp.exp(scores - summit)  4.36 us

profile of v1, /device:TPU:9, one launch (start us, length us, event | category | flops | bytes accessed | tf_op | source)
XLA Modules:
  0.0 213.6 jit_solution(18125864906317528253)
XLA Ops:
  1.3 0.7 fusion.39
  2.7 1.4 gather_fusion.1
  4.8 0.8 or_and_fusion
  5.6 1.5 pad_maximum_fusion.1.down_ref
  7.1 0.9 fusion.32
  8.0 0.7 broadcast_in_dim.40
  8.8 1.2 broadcast_in_dim.39.mask_ref
  9.9 2.3 %constant_dynamic-slice_fusion.x_ref = bf16[512,1024]{1,0:T(8,128)(2,1)} fusion(bf16[512,4096]{1,0:T(8,128)(2,1)} %x_hbm.1, s32[]{:T(128)S(6)} %select_n.17), kind=kLoop, calls=%fused_computation.77 | loop fusion | bytes 2097156 | tf_op jit(solution)/shard_map/dynamic_slice | solution.py:547
  12.2 0.7 reshape.196
  13.0 1.5 copy.37
  14.4 133.8 %project.1 = (f32[512,1536]{1,0:T(8,128)}, bf16[512,64]{1,0:T(8,128)(2,1)}, bf16[4,32,1024]{2,1,0:T(8,128)(2,1)}, bf16[4,32,256]{2,1,0:T(8,128)(2,1)}) custom-call(s32[4]{0:T(128)} %copy-done.11, s32[4]{0:T(128)} %copy-done.13, f32[4]{0:T(128)} %convert_divide_fusion.scale_ref, bf16[512,4096]{1,0:T(8,128)(2,1)} %x_hbm.1, bf16[1024,1024]{1,0:T(8,128)(2,1)} %wq_hbm.1, ...), custom_call_target="tpu_custom_call" | custom-call | tf_op jit(solution)/shard_map/project/pallas_call | solution.py:348
  148.2 1.1 slice.72
  149.3 0.8 reshape.195
  150.1 1.1 fusion.51
  151.1 1.1 slice.40
  152.2 1.7 slice_bitcast_fusion
  154.7 0.8 subtract_convert_fusion.1
  156.3 0.9 subtract_convert_fusion.2
  157.5 4.4 %fusion.52 = (f32[4,2,4,128]{3,2,1,0:T(4,128)}, f32[4,2,4,128,128]{3,4,2,1,0:T(8,128)}) fusion(pred[4,128,128]{1,2,0:T(8,128)(4,1)} %or_and_fusion, bf16[4,128,2,4,64]{4,1,3,2,0:T(8,128)(2,1)S(1)} %bitcast.97, bf16[4,128,2,4,64]{4,1,3,2,0:T(8,128)(2,1)S(1)} %bitcast.96, bf16[4,128,2,64]{3,1,2,0:T(8,128)(2,1)} %get-tuple-element.25, ...), kind=kOutput, calls=%fused_computation.87 | convolution fusion | flops 138936448 | bytes 3489792 | tf_op jit(solution)/shard_map/sub | solution.py:48
  161.9 2.2 %fusion.5 = bf16[4,2,128,128]{3,2,1,0:T(8,128)(2,1)S(1)} fusion(bf16[4,128,2,4,128]{1,4,3,2,0:T(8,128)(2,1)S(1)} %copy-done.2, pred[4,128]{1,0:T(4,128)(4,1)S(1)} %add_compare_fusion, f32[4,2,4,128,128]{3,4,2,1,0:T(8,128)} %get-tuple-element.36, f32[4,2,4,128]{3,2,1,0:T(4,128)} %get-tuple-element.35), kind=kOutput, calls=%fused_computation.18 | convolution fusion | flops 135921664 | bytes 3424768 | tf_op jit(solution)/shard_map/nkgts,ntkge->nske/dot_general | solution.py:59
  164.2 0.8 fusion.7
  167.1 0.7 convolution_multiply_fusion
  167.8 1.2 fusion.49
  169.0 1.9 copy.66
  170.9 1.9 copy.65
  172.9 2.2 %subtract_convert_fusion = (bf16[4,128,8,64]{3,2,1,0:T(8,128)(2,1)S(1)}, bf16[4,128,8,64]{3,2,1,0:T(8,128)(2,1)S(1)}) fusion(f32[4,128,8,64]{3,2,1,0:T(8,128)S(1)} %copy.66, f32[4,128,8,64]{3,2,1,0:T(8,128)} %copy.65, f32[128,64]{1,0:T(8,128)S(1)} %copy-done.3, f32[128,64]{1,0:T(8,128)S(1)} %get-tuple-element.34), kind=kLoop, calls=%fused_computation.10 | loop fusion | flops 2097152 | bytes 3211264 | tf_op jit(solution)/shard_map/convert.3
  177.5 0.8 copy.82.upq_ref
  178.3 0.8 copy.46
  179.1 29.9 %reduce_grads.1 = (f32[64,1024]{1,0:T(8,128)}, f32[32,1024]{1,0:T(8,128)}, f32[32,256]{1,0:T(8,128)}) custom-call(bf16[512,1024]{1,0:T(8,128)(2,1)} %constant_dynamic-slice_fusion.x_ref, bf16[4,512,64]{2,1,0:T(8,128)(2,1)} %broadcast_in_dim.39.mask_ref, f32[512,64]{1,0:T(8,128)} %bitcast.95, bf16[512,64]{1,0:T(8,128)(2,1)} %bitcast.100, ...), custom_call_target="tpu_custom_call" | custom-call | tf_op jit(solution)/shard_map/reduce_grads/pallas_call | solution.py:492
  209.0 1.7 slice_bitcast_fusion.1
  210.7 1.6 copy.90
  212.3 1.4 copy.91
  (58 shorter events, 7.7 us)
Async XLA Ops:
  0.6 1.4 copy-start
  2.7 10.3 %copy-start.11 = (s32[4]{0:T(128)}, s32[4]{0:T(128)S(1)}, u32[]{:S(2)}) copy-start(s32[4]{0:T(128)S(1)} %gather_fusion) | copy-start | bytes 52
  2.7 9.5 %copy-start.1 = (bf16[512,1024]{1,0:T(8,128)(2,1)S(1)}, bf16[512,1024]{1,0:T(8,128)(2,1)}, u32[]{:S(2)}) copy-start(bf16[512,1024]{1,0:T(8,128)(2,1)} %param.25) | copy-start | bytes 3145732
  4.0 8.9 %copy-start.13 = (s32[4]{0:T(128)}, s32[4]{0:T(128)S(1)}, u32[]{:S(2)}) copy-start(s32[4]{0:T(128)S(1)} %gather_fusion.1) | copy-start | bytes 52
  157.5 4.4 %copy-start.2 = (bf16[4,128,2,4,128]{1,4,3,2,0:T(8,128)(2,1)S(1)}, bf16[4,128,2,4,128]{1,4,3,2,0:T(8,128)(2,1)}, u32[]{:S(2)}) copy-start(bf16[4,128,2,4,128]{1,4,3,2,0:T(8,128)(2,1)} %copy.37) | copy-start | bytes 3145732
  161.9 2.3 %copy-start.9 = (bf16[4,32,256]{2,1,0:T(8,128)(2,1)S(1)}, bf16[4,32,256]{2,1,0:T(8,128)(2,1)}, u32[]{:S(2)}) copy-start(bf16[4,32,256]{2,1,0:T(8,128)(2,1)} %get-tuple-element.13) | copy-start | bytes 196612
  161.9 2.3 %copy-start.10 = (f32[4]{0:T(128)S(1)}, f32[4]{0:T(128)}, u32[]{:S(2)}) copy-start(f32[4]{0:T(128)} %convert_divide_fusion.scale_ref) | copy-start | bytes 52
  161.9 3.3 %copy-start.12 = (s32[4]{0:T(128)S(1)}, s32[4]{0:T(128)}, u32[]{:S(2)}) copy-start(s32[4]{0:T(128)} %copy-done.11) | copy-start | bytes 52
  161.9 4.2 %copy-start.5 = (bf16[4,128,2,128]{3,2,1,0:T(2,128)(2,1)S(1)}, bf16[4,128,2,128]{3,2,1,0:T(2,128)(2,1)}, u32[]{:S(2)}) copy-start(bf16[4,128,2,128]{3,2,1,0:T(2,128)(2,1)} %reshape.195) | copy-start | bytes 786436
  161.9 4.2 %copy-start.14 = (f32[4,2,4,128,128]{3,4,2,1,0:T(8,128)S(1)}, f32[4,2,4,128,128]{3,4,2,1,0:T(8,128)}, u32[]{:S(2)}) copy-start(f32[4,2,4,128,128]{3,4,2,1,0:T(8,128)} %get-tuple-element.36) | copy-start | bytes 6291460
  161.9 4.2 %copy-start.15 = (f32[4,2,4,128]{3,2,1,0:T(4,128)S(1)}, f32[4,2,4,128]{3,2,1,0:T(4,128)}, u32[]{:S(2)}) copy-start(f32[4,2,4,128]{3,2,1,0:T(4,128)} %get-tuple-element.35) | copy-start | bytes 49156
  166.1 1.0 copy-start.6
  166.1 1.0 copy-start.7
  170.9 2.0 copy-start.3
  175.1 1.1 copy-start.4
  176.2 2.1 copy-start.8

commit v2 on v1

--- a/solution.py
+++ b/solution.py
@@ -2,6 +2,7 @@
 
 import jax
 import jax.numpy as jnp
+import numpy as np
 from jax import lax
 from jax.experimental import pallas as pl
 from jax.experimental.pallas import tpu as pltpu
@@ -19,45 +20,13 @@
 
 def rope_tables(length, width):
     halfway = width // 2
-    spread = rope_theta ** (-2.0 * jnp.arange(halfway, dtype=jnp.float32) / width)
-    angle = jnp.arange(length, dtype=jnp.float32)[:, None] * spread[None, :]
-    return (jnp.cos(angle), jnp.sin(angle))
-
-
-def rotate(value_matrix, cosine, sine):
-    halfway = value_matrix.shape[-1] // 2
-    first = value_matrix[..., :halfway]
-    second = value_matrix[..., halfway:]
-    cos_grid = cosine[:, None, :]
-    sin_grid = sine[:, None, :]
-    return jnp.concatenate(
-        [first * cos_grid - second * sin_grid, second * cos_grid + first * sin_grid], axis=-1
-    )
-
-
-def attention_grads(queries, keys, value_matrix, dout, allowed, group):
-    request_block_count, length, heads, depth = queries.shape
-    kv_heads = keys.shape[2]
-    grouped_q = queries.reshape(request_block_count, length, kv_heads, group, depth)
-    grouped_d = dout.reshape(request_block_count, length, kv_heads, group, depth)
-    scores = jnp.einsum(
-        "ntkge,nske->nkgts", grouped_q, keys, preferred_element_type=jnp.float32
-    ) * depth ** (-0.5)
-    scores = jnp.where(allowed[:, None, None], scores, -1e30)
-    summit = jnp.max(scores, axis=-1, keepdims=True)
-    expo = jnp.exp(scores - summit)
-    probs = expo / jnp.sum(expo, axis=-1, keepdims=True)
-    dprobs = jnp.einsum(
-        "ntkge,nske->nkgts", grouped_d, value_matrix, preferred_element_type=jnp.float32
-    )
-    dscores = probs * (dprobs - jnp.sum(dprobs * probs, axis=-1, keepdims=True))
-    dscore_b = dscores.astype(jnp.bfloat16)
-    dquery = jnp.einsum(
-        "nkgts,nske->ntkge", dscore_b, keys, preferred_element_type=jnp.float32
-    ) * depth ** (-0.5)
-    prob_b = probs.astype(jnp.bfloat16)
-    dvalue = jnp.einsum("nkgts,ntkge->nske", prob_b, grouped_d, preferred_element_type=jnp.float32)
-    return (dquery.reshape(request_block_count, length, heads, depth), dvalue)
+    spread = rope_theta ** (-2.0 * np.arange(halfway, dtype=np.float32) / width)
+    angle = np.arange(length, dtype=np.float32)[:, None] * spread.astype(np.float32)[None, :]
+    return np.cos(angle).astype(np.float32), np.sin(angle).astype(np.float32)
+
+
+def scale_of(rank):
+    return (adapter_alpha_factor / jnp.full((1, 128), rank, jnp.int32).astype(jnp.float32))[:, :1]
 
 
 def greet(axes):
@@ -79,9 +48,9 @@
 
 def project_kernel(
     pieces,
+    block_ref,
     slot_ref,
     rank_ref,
-    scale_ref,
     x_hbm,
     wq_hbm,
     wk_hbm,
@@ -223,7 +192,7 @@
     mine = pl.ds(pl.multiple_of(t * width, 128), width)
     for b in range(block_count):
         span = pl.ds(b * REQUEST_ROWS, REQUEST_ROWS)
-        slot = slot_ref[b]
+        slot = slot_ref[block_ref[b, 0]]
         parts[t, span, :] = lax.dot_general(
             x_ref[span, mine],
             down_all[slot],
@@ -282,7 +251,8 @@
         part_copy(j, True).wait_recv()
     for b in range(block_count):
         span = pl.ds(b * REQUEST_ROWS, REQUEST_ROWS)
-        rank = rank_ref[b]
+        rank = rank_ref[block_ref[b, 0]]
+        scale = scale_of(rank)
         total = parts[0, span, :]
         for j in range(1, nt):
             total = total + parts[j, span, :]
@@ -290,10 +260,10 @@
         lane = jnp.where(lane >= R, lane - R, lane)
         u = jnp.where(lane < rank, total, 0.0).astype(jnp.bfloat16)
         u_ref[span, :] = u
-        acc_ref[span, :qcols] += scale_ref[b] * jnp.dot(
+        acc_ref[span, :qcols] += scale * jnp.dot(
             u[:, :R], bq_sel_ref[b], preferred_element_type=jnp.float32
         )
-        acc_ref[span, qcols + kcols :] += scale_ref[b] * jnp.dot(
+        acc_ref[span, qcols + kcols :] += scale * jnp.dot(
             u[:, R:], bv_sel_ref[b], preferred_element_type=jnp.float32
         )
 
@@ -332,7 +302,7 @@
                     y_copy(s, p, j, False).wait_send()
 
 
-def project(tokens, w_query, w_key, w_value, down, b_query, b_value, slots, ranks, scales):
+def project(tokens, w_query, w_key, w_value, down, b_query, b_value, blocks_of, slots, ranks):
     n, ng, nt = lax.axis_size("dp"), lax.axis_size("groups"), lax.axis_size("tensor")
     rows = tokens.shape[0]
     depth, qcols = w_query.shape
@@ -376,19 +346,23 @@
             collective_id=0, has_side_effects=True, vmem_limit_bytes=60 * 1024 * 1024
         ),
         name="project",
-    )(slots, ranks, scales, tokens, w_query, w_key, w_value, down, b_query, b_value)
+    )(blocks_of, slots, ranks, tokens, w_query, w_key, w_value, down, b_query, b_value)
 
 
 def reduce_kernel(
-    x_ref,
-    mask_ref,
-    keep_ref,
+    block_ref,
+    slot_ref,
+    rank_ref,
+    x_hbm,
     part_ref,
     upq_ref,
     upv_ref,
     low_out,
     upq_out,
     upv_out,
+    x_ref,
+    back_ref,
+    x_sem,
     backs,
     low_send,
     low_got,
@@ -401,6 +375,12 @@
 ):
     n, nt = lax.axis_size("dp"), lax.axis_size("tensor")
     me, t = lax.axis_index("dp"), lax.axis_index("tensor")
+    width = x_ref.shape[1]
+    block_count = x_ref.shape[0] // REQUEST_ROWS
+    x_copy = pltpu.make_async_copy(
+        x_hbm.at[:, pl.ds(pl.multiple_of(t * width, 128), width)], x_ref, x_sem
+    )
+    x_copy.start()
     greet(("dp", "tensor"))
 
     def back_copy(j, arriving):
@@ -442,12 +422,28 @@
     total = backs[0].astype(jnp.float32)
     for j in range(1, nt):
         total = total + backs[j].astype(jnp.float32)
-    back = (total * keep_ref[...]).astype(jnp.bfloat16)
+    lane = lax.broadcasted_iota(jnp.int32, (REQUEST_ROWS, 2 * R), 1)
+    lane = jnp.where(lane >= R, lane - R, lane)
+    for b in range(block_count):
+        span = pl.ds(b * REQUEST_ROWS, REQUEST_ROWS)
+        kept = total[b * REQUEST_ROWS : (b + 1) * REQUEST_ROWS]
+        back_ref[span, :] = jnp.where(lane < rank_ref[block_ref[b, 0]], kept, 0.0)
+    x_copy.wait()
 
     @pl.loop(1, n + 1)
     def _(j):
         a = lax.rem(me + j, n)
-        chosen = (mask_ref[a] * back).astype(jnp.bfloat16)
+        chosen = jnp.concatenate(
+            [
+                jnp.where(
+                    jnp.full((REQUEST_ROWS, 2 * R), slot_ref[block_ref[b, 0]], jnp.int32) == a,
+                    back_ref[pl.ds(b * REQUEST_ROWS, REQUEST_ROWS), :],
+                    0.0,
+                )
+                for b in range(block_count)
+            ],
+            axis=0,
+        ).astype(jnp.bfloat16)
         low_send[a] = lax.dot_general(
             chosen, x_ref[...], (((0,), (0,)), ((), ())), preferred_element_type=jnp.float32
         ).astype(jnp.bfloat16)
@@ -483,9 +479,11 @@
             grad_copy(i, src, dst, j, False).wait_send()
 
 
-def reduce_grads(x_local, mask, keep, part, up_q, up_v):
+def reduce_grads(tokens, width, blocks_of, slots, ranks, part, up_q, up_v):
     n, nt = lax.axis_size("dp"), lax.axis_size("tensor")
-    rows, width = x_local.shape
+    rows = tokens.shape[0]
+    smem = pl.BlockSpec(memory_space=pltpu.SMEM)
+    hbm = pl.BlockSpec(memory_space=pltpu.HBM)
     vmem = pl.BlockSpec(memory_space=pltpu.VMEM)
     dma = pltpu.SemaphoreType.DMA
     low_shape = (n, 2 * R, width)
@@ -496,9 +494,12 @@
             jax.ShapeDtypeStruct(up_q.shape[1:], jnp.float32),
             jax.ShapeDtypeStruct(up_v.shape[1:], jnp.float32),
         ),
-        in_specs=[vmem] * 6,
+        in_specs=[smem] * 3 + [hbm] + [vmem] * 3,
         out_specs=(vmem,) * 3,
         scratch_shapes=[
+            pltpu.VMEM((rows, width), jnp.bfloat16),
+            pltpu.VMEM((rows, 2 * R), jnp.float32),
+            dma,
             pltpu.VMEM((nt,) + part.shape, jnp.bfloat16),
             pltpu.VMEM(low_shape, jnp.bfloat16),
             pltpu.VMEM(low_shape, jnp.bfloat16),
@@ -513,7 +514,149 @@
             collective_id=1, has_side_effects=True, vmem_limit_bytes=60 * 1024 * 1024
         ),
         name="reduce_grads",
-    )(x_local, mask, keep, part, up_q, up_v)
+    )(blocks_of, slots, ranks, tokens, part, up_q, up_v)
+
+def attend_kernel(
+    group,
+    block_ref,
+    slot_ref,
+    rank_ref,
+    live_ref,
+    cos_ref,
+    sin_ref,
+    q_ref,
+    kv_ref,
+    u_ref,
+    bq_ref,
+    bv_ref,
+    d_ref,
+    part_ref,
+    upq_ref,
+    upv_ref,
+    gq_ref,
+    gv_ref,
+    upq_sum,
+    upv_sum,
+):
+    b = pl.program_id(0)
+    kcols = kv_ref.shape[1] // 2
+    kv_heads = kcols // HD
+    adapter = block_ref[b, 0]
+    slot = slot_ref[adapter]
+    scale = scale_of(rank_ref[adapter])
+    live = live_ref[0] - b * REQUEST_ROWS
+
+    @pl.when(b == 0)
+    def _():
+        upq_sum[...] = jnp.zeros_like(upq_sum)
+        upv_sum[...] = jnp.zeros_like(upv_sum)
+
+    cosine, sine = cos_ref[...], sin_ref[...]
+    dims = (REQUEST_ROWS, REQUEST_ROWS)
+    query_at = lax.broadcasted_iota(jnp.int32, dims, 0)
+    key_at = lax.broadcasted_iota(jnp.int32, dims, 1)
+    allowed = (key_at <= query_at) & ((key_at < live) | (key_at == query_at))
+    allowed = jnp.concatenate([allowed.astype(jnp.float32)] * group, axis=0) > 0.5
+    live_rows = lax.broadcasted_iota(jnp.int32, (REQUEST_ROWS, HD), 0) < live
+
+    def turn(item, sign):
+        return item * cosine + pltpu.roll(item, HD // 2, 1) * (sign * sine)
+
+    def dot(a, c, left, right):
+        return lax.dot_general(
+            a, c, (((left,), (right,)), ((), ())), preferred_element_type=jnp.float32
+        )
+
+    for k in range(kv_heads):
+        keys = turn(kv_ref[:, k * HD : (k + 1) * HD], 1.0).astype(jnp.bfloat16)
+        values = kv_ref[:, kcols + k * HD : kcols + (k + 1) * HD].astype(jnp.bfloat16)
+        heads = [pl.ds((k * group + i) * HD, HD) for i in range(group)]
+        queries = jnp.concatenate(
+            [turn(q_ref[:, h], 1.0).astype(jnp.bfloat16) for h in heads], axis=0
+        )
+        dout = jnp.concatenate(
+            [
+                jnp.where(live_rows, d_ref[:, h].astype(jnp.float32), 0.0).astype(jnp.bfloat16)
+                for h in heads
+            ],
+            axis=0,
+        )
+        scores = dot(queries, keys, 1, 1) * HD ** (-0.5)
+        scores = jnp.where(allowed, scores, -1e30)
+        expo = jnp.exp(scores - jnp.max(scores, axis=-1, keepdims=True))
+        probs = expo / jnp.sum(expo, axis=-1, keepdims=True)
+        dprobs = dot(dout, values, 1, 1)
+        dscores = probs * (dprobs - jnp.sum(dprobs * probs, axis=-1, keepdims=True))
+        dquery = dot(dscores.astype(jnp.bfloat16), keys, 1, 0) * HD ** (-0.5)
+        for i, h in enumerate(heads):
+            rows = dquery[i * REQUEST_ROWS : (i + 1) * REQUEST_ROWS]
+            gq_ref[:, h] = turn(rows, -1.0).astype(jnp.bfloat16)
+        gv_ref[:, k * HD : (k + 1) * HD] = dot(probs.astype(jnp.bfloat16), dout, 0, 0).astype(
+            jnp.bfloat16
+        )
+    u = u_ref[...]
+    upq_sum[slot] += scale * dot(u[:, :R], gq_ref[...], 0, 0)
+    upv_sum[slot] += scale * dot(u[:, R:], gv_ref[...], 0, 0)
+    part_ref[...] = (
+        scale
+        * jnp.concatenate(
+            [dot(gq_ref[...], bq_ref[0], 1, 1), dot(gv_ref[...], bv_ref[0], 1, 1)], axis=-1
+        )
+    ).astype(jnp.bfloat16)
+
+    @pl.when(b == pl.num_programs(0) - 1)
+    def _():
+        upq_ref[...] = upq_sum[...].astype(jnp.bfloat16)
+        upv_ref[...] = upv_sum[...].astype(jnp.bfloat16)
+
+
+def attend(full, low_rank, up_query, up_value, d_heads, blocks_of, slots, ranks, live):
+    slot_count = slots.shape[0]
+    rows, qcols = d_heads.shape
+    kcols = up_value.shape[2]
+    group = qcols // kcols
+    cosine, sine = rope_tables(REQUEST_ROWS, HD)
+    cosine = np.concatenate([cosine, cosine], axis=-1)
+    sine = np.concatenate([-sine, sine], axis=-1)
+    smem = pl.BlockSpec(memory_space=pltpu.SMEM)
+    table = pl.BlockSpec((REQUEST_ROWS, HD), lambda b: (0, 0))
+    upq_shape = (slot_count, R, qcols)
+    upv_shape = (slot_count, R, kcols)
+    ratio = qcols // (2 * kcols)
+    return pl.pallas_call(
+        functools.partial(attend_kernel, group),
+        grid=(rows // REQUEST_ROWS,),
+        out_shape=(
+            jax.ShapeDtypeStruct((rows, 2 * R), jnp.bfloat16),
+            jax.ShapeDtypeStruct(upq_shape, jnp.bfloat16),
+            jax.ShapeDtypeStruct(upv_shape, jnp.bfloat16),
+        ),
+        in_specs=[smem] * 4
+        + [
+            table,
+            table,
+            pl.BlockSpec((REQUEST_ROWS, qcols), lambda b: (b, 0)),
+            pl.BlockSpec((REQUEST_ROWS, 2 * kcols), lambda b: (b, ratio)),
+            pl.BlockSpec((REQUEST_ROWS, 2 * R), lambda b: (b, 0)),
+            pl.BlockSpec((1, R, qcols), lambda b: (b, 0, 0)),
+            pl.BlockSpec((1, R, kcols), lambda b: (b, 0, 0)),
+            pl.BlockSpec((REQUEST_ROWS, qcols), lambda b: (b, 0)),
+        ],
+        out_specs=(
+            pl.BlockSpec((REQUEST_ROWS, 2 * R), lambda b: (b, 0)),
+            pl.BlockSpec(upq_shape, lambda b: (0, 0, 0)),
+            pl.BlockSpec(upv_shape, lambda b: (0, 0, 0)),
+        ),
+        scratch_shapes=[
+            pltpu.VMEM((REQUEST_ROWS, qcols), jnp.bfloat16),
+            pltpu.VMEM((REQUEST_ROWS, kcols), jnp.bfloat16),
+            pltpu.VMEM(upq_shape, jnp.float32),
+            pltpu.VMEM(upv_shape, jnp.float32),
+        ],
+        name="attend",
+    )(
+        blocks_of, slots, ranks, live, cosine, sine, full, full, low_rank, up_query, up_value, d_heads
+    )
 
 
 def on_device(
@@ -531,101 +674,18 @@
     live_tokens,
     d_heads,
 ):
-    row_count = tokens.shape[0]
-    request_block_count = row_count // REQUEST_ROWS
-    local_width = a_query.shape[1]
-    query_column_count = w_query.shape[1]
-    value_column_count = w_key.shape[1]
-    local_heads = query_column_count // HD
-    local_kv = value_column_count // HD
-    group = local_heads // local_kv
-    dp_count = lax.axis_size("dp")
-    owned = a_query.shape[0]
-    adapter_count = owned * dp_count
-    cosine, sine = rope_tables(REQUEST_ROWS, HD)
-    column_start = lax.axis_index("tensor") * local_width
-    tok_local = lax.dynamic_slice_in_dim(tokens, column_start, local_width, 1)
-    block_ids = block_adapter[:, 0]
-    slot_ids = adapter_slot[block_ids]
-    rank_index_list = adapter_ranks[block_ids]
-    scales = adapter_alpha_factor / rank_index_list.astype(jnp.float32)
-    adapter_scale = scales[:, None, None]
-    keep = (jnp.arange(R, dtype=jnp.int32)[None, :] < rank_index_list[:, None]).astype(jnp.float32)
+    width = a_query.shape[1]
     down = jnp.concatenate([a_query[0].T, a_value[0].T], axis=0)
-    full, low_rank, selected_query_up, selected_value_up = project(
+    full, low_rank, up_query, up_value = project(
         tokens, w_query, w_key, w_value, down, b_query[0], b_value[0],
-        slot_ids, rank_index_list, scales,
+        block_adapter, adapter_slot, adapter_ranks,
     )
-    shape3 = (request_block_count, REQUEST_ROWS, -1)
-    query_down_weight = low_rank[:, :R].reshape(shape3)
-    value_down_weight = low_rank[:, R:].reshape(shape3)
-    queries = rotate(
-        full[:, :query_column_count].reshape(request_block_count, REQUEST_ROWS, local_heads, HD),
-        cosine, sine,
-    ).astype(jnp.bfloat16)
-    keys = rotate(
-        full[:, query_column_count : query_column_count + value_column_count].reshape(
-            request_block_count, REQUEST_ROWS, local_kv, HD
-        ),
-        cosine, sine,
-    ).astype(jnp.bfloat16)
-    value_matrix = full[:, query_column_count + value_column_count :].astype(jnp.bfloat16)
-    value_matrix = value_matrix.reshape(request_block_count, REQUEST_ROWS, local_kv, HD)
-    position = jnp.arange(REQUEST_ROWS, dtype=jnp.int32)
-    causal = position[None, :] <= position[:, None]
-    diagonal = position[None, :] == position[:, None]
-    row_index = jnp.arange(row_count, dtype=jnp.int32).reshape(request_block_count, REQUEST_ROWS)
-    live = row_index < live_tokens[0]
-    allowed = causal[None] & (live[:, None, :] | diagonal[None])
-    dout = jnp.where(
-        live[:, :, None],
-        d_heads.reshape(request_block_count, REQUEST_ROWS, query_column_count),
-        jnp.zeros((), jnp.bfloat16),
+    part, up_q, up_v = attend(
+        full, low_rank, up_query, up_value, d_heads,
+        block_adapter, adapter_slot, adapter_ranks, live_tokens,
     )
-    dquery, dvalue = attention_grads(
-        queries,
-        keys,
-        value_matrix,
-        dout.reshape(request_block_count, REQUEST_ROWS, local_heads, HD),
-        allowed,
-        group,
-    )
-    grad_q = (
-        rotate(dquery, cosine, -sine)
-        .reshape(request_block_count, REQUEST_ROWS, query_column_count)
-        .astype(jnp.bfloat16)
-    )
-    grad_v = dvalue.reshape(request_block_count, REQUEST_ROWS, value_column_count).astype(
-        jnp.bfloat16
-    )
-    up_q = adapter_scale * jnp.einsum(
-        "ntr,ntc->nrc", query_down_weight, grad_q, preferred_element_type=jnp.float32
-    )
-    up_v = adapter_scale * jnp.einsum(
-        "ntr,ntc->nrc", value_down_weight, grad_v, preferred_element_type=jnp.float32
-    )
-    part_back_q = adapter_scale * jnp.einsum(
-        "ntc,nrc->ntr", grad_q, selected_query_up, preferred_element_type=jnp.float32
-    )
-    part_back_v = adapter_scale * jnp.einsum(
-        "ntc,nrc->ntr", grad_v, selected_value_up, preferred_element_type=jnp.float32
-    )
-    part_back = jnp.concatenate([part_back_q, part_back_v], axis=-1)
-    part_back = part_back.reshape(row_count, 2 * R).astype(jnp.bfloat16)
-    chosen = jnp.arange(adapter_count, dtype=jnp.int32)[:, None] == slot_ids[None, :]
-    onehot = chosen.astype(jnp.float32)
-    placed_q, placed_v = (
-        jnp.einsum("an,nxy->axy", onehot, item).astype(jnp.bfloat16) for item in (up_q, up_v)
-    )
-    row_mask = jnp.broadcast_to(
-        chosen[:, :, None, None], (adapter_count, request_block_count, REQUEST_ROWS, 2 * R)
-    ).reshape(adapter_count, row_count, 2 * R).astype(jnp.bfloat16)
-    row_keep = jnp.broadcast_to(
-        jnp.concatenate([keep, keep], axis=-1)[:, None, :],
-        (request_block_count, REQUEST_ROWS, 2 * R),
-    ).reshape(row_count, 2 * R)
     low, grad_bq, grad_bv = reduce_grads(
-        tok_local, row_mask, row_keep, part_back, placed_q, placed_v
+        tokens, width, block_adapter, adapter_slot, adapter_ranks, part, up_q, up_v
     )
     return (low[:R].T[None], grad_bq[None], low[R:].T[None], grad_bv[None])
 

time: 214 us -> 182 us (0.85)
  local copies, waits for them, and re-layouts: 29 us -> 5.94 us
  matrix products: 10.2 us -> 0 us
  Pallas kernels: 164 us -> 173 us
  other arithmetic: 9.1 us -> 1.53 us
    pallas_call x0 -> x1, Pallas kernels: none -> 9.92 us  [attend(): pl.pallas_call(functools.partial(attend_kernel, group), grid=(rows // REQ...]
    dot_general x9 -> x0, matrix products: 5.83 us -> none  [the longest x1 2.21 us: attention_grads(): jnp.einsum('nkgts,ntkge->nske', prob_b, grouped_d, preferred_element_type...]
    unnamed x40 -> x3, local copies, waits for them, and re-layouts: 9.69 us -> 4.25 us
    slice x5 -> x0, local copies, waits for them, and re-layouts: 5.02 us -> none  [the longest x1 1.19 us: rotate(): second = value_matrix[..., halfway:]]
    sub x1 -> x0, matrix products: 4.36 us -> none  [attention_grads(): expo = jnp.exp(scores - summit)]
    another operation x3 -> x0, other arithmetic: 3.94 us -> none
    reshape x4 -> x0, local copies, waits for them, and re-layouts: 3.27 us -> none  [the longest x2 2.21 us: on_device(): d_heads.reshape(request_block_count, REQUEST_ROWS, query_column_count)]
    dynamic_slice x1 -> x0, local copies, waits for them, and re-layouts: 2.28 us -> none  [on_device(): tok_local = lax.dynamic_slice_in_dim(tokens, column_start, local_width, 1)]
where the time goes in v2:
time: 182 us
  Pallas kernels  173 us (95%)
  local copies, waits for them, and re-layouts  5.94 us (3%)
    pallas_call x1, Pallas kernels, project(): pl.pallas_call(functools.partial(project_kernel, pieces), out_shape=(jax....  134 us
    pallas_call x1, Pallas kernels, reduce_grads(): pl.pallas_call(reduce_kernel, out_shape=(jax.ShapeDtypeStruct(low_shape[1...  29.3 us
    pallas_call x1, Pallas kernels, attend(): pl.pallas_call(functools.partial(attend_kernel, group), grid=(rows // REQ...  9.92 us
    unnamed x3, local copies, waits for them, and re-layouts  4.25 us

profile of v2, /device:TPU:9, one launch (start us, length us, event | category | flops | bytes accessed | tf_op | source)
XLA Modules:
  0.0 181.8 jit_solution(1012971922989847091)
XLA Ops:
  1.3 1.3 copy.21.block_ref
  2.6 1.5 pad_maximum_fusion.down_ref
  4.1 133.7 %project.1 = (f32[512,1536]{1,0:T(8,128)}, bf16[512,64]{1,0:T(8,128)(2,1)}, bf16[4,32,1024]{2,1,0:T(8,128)(2,1)}, bf16[4,32,256]{2,1,0:T(8,128)(2,1)}) custom-call(s32[4,1]{1,0:T(4,128)} %copy.21.block_ref, s32[4]{0:T(128)} %slot_ref.5, s32[4]{0:T(128)} %rank_ref.5, bf16[512,4096]{1,0:T(8,128)(2,1)} %x_hbm.3, bf16[1024,1024]{1,0:T(8,128)(2,1)} %wq_hbm.1, ...), custom_call_target="tpu_custom_call" | custom-call | tf_op jit(solution)/shard_map/project/pallas_call | solution.py:318
  137.9 9.9 %attend.1 = (bf16[512,64]{1,0:T(8,128)(2,1)}, bf16[4,32,1024]{2,1,0:T(8,128)(2,1)}, bf16[4,32,256]{2,1,0:T(8,128)(2,1)}) custom-call(s32[4,1]{1,0:T(4,128)} %copy.21.block_ref, s32[4]{0:T(128)} %slot_ref.5, s32[4]{0:T(128)} %rank_ref.5, s32[1]{0:T(128)S(6)} %copy.24.live_ref, f32[128,128]{1,0:T(8,128)} %constant.4.clone.cos_ref, ...), custom_call_target="tpu_custom_call" | custom-call | tf_op jit(solution)/shard_map/attend/pallas_call | solution.py:626
  147.8 29.3 %reduce_grads.1 = (f32[64,1024]{1,0:T(8,128)}, f32[32,1024]{1,0:T(8,128)}, f32[32,256]{1,0:T(8,128)}) custom-call(s32[4,1]{1,0:T(4,128)} %copy.21.block_ref, s32[4]{0:T(128)} %slot_ref.5, s32[4]{0:T(128)} %rank_ref.5, bf16[512,4096]{1,0:T(8,128)(2,1)} %x_hbm.3, bf16[512,64]{1,0:T(8,128)(2,1)} %get-tuple-element.18.part_ref, ...), custom_call_target="tpu_custom_call" | custom-call | tf_op jit(solution)/shard_map/reduce_grads/pallas_call | solution.py:490
  177.2 1.7 slice_bitcast_fusion
  178.8 1.6 copy.25
  180.4 1.4 copy.26
